TPU v7x, 32 devices: a whole 2x2x4 slice. The times are simulated.
32 devices in a mesh: dp: 16 (over z, x, core), head: 2 (over y).
Axes of the slice: x: 2, y: 2, z: 4, core: 2. Of those that a mesh axis runs over, the one named last changes fastest.
Arguments:
- frames_in: bfloat16 [16, 2, 320, 2560], P('dp', 'head'), may hold values from -6 to 6
- ln1_gain: float32 [1280], replicated, may hold values from 0.25 to 1.75
- ln1_bias: float32 [1280], replicated, may hold values from -3 to 3
- qkv_weight: bfloat16 [1280, 3, 1024], P('dp', None, 'head'), may hold values from -0.1875 to 0.1875
- qv_bias: float32 [2, 1024], P(None, 'head'), may hold values from -3 to 3
- out_weight: bfloat16 [1024, 1280], P(('head', 'dp')), may hold values from -0.1875 to 0.1875
- out_bias: float32 [1280], P('head'), may hold values from -3 to 3
- ln2_gain: float32 [1280], replicated, may hold values from 0.25 to 1.75
- ln2_bias: float32 [1280], replicated, may hold values from -3 to 3
- fc1_weight: bfloat16 [1280, 5120], P('dp', 'head'), may hold values from -0.15625 to 0.15625
- fc1_bias: float32 [5120], P('head'), may hold values from -3 to 3
- fc2_weight: bfloat16 [5120, 1280], P(('head', 'dp')), may hold values from -0.078125 to 0.078125
- fc2_bias: float32 [1280], P('head'), may hold values from -3 to 3
- server_of_clip: int32 [16], replicated, may hold values from 0 to 7
Outputs:
- encoded: bfloat16 [16, 2, 320, 2560], P('dp', 'head')
All inputs are finite; a program needn't handle non-finite values.
Results may differ from a plain program's by a relative error of at most 0.014.
Values may be sent and summed in bfloat16 or wider, within the bound.
A program may use at most 64 MiB of HBM per device.

v0:
```python
import jax
import jax.numpy as jnp
from jax import lax
from jax.sharding import PartitionSpec as P

HDIM = 64
epsilon = 1e-05


def layer_norm(matrix, gain_row, shift_row):
    floats = matrix.astype(jnp.float32)
    center = jnp.mean(floats, axis=-1, keepdims=True)
    spread = jnp.mean(jnp.square(floats - center), axis=-1, keepdims=True)
    return ((floats - center) * lax.rsqrt(spread + epsilon) * gain_row + shift_row).astype(
        jnp.bfloat16
    )


def normalize(residual_in, gain_row, shift_row):
    whole_rows = lax.all_gather(residual_in, "head", axis=1, tiled=True)
    return layer_norm(whole_rows, gain_row, shift_row)


def attend(queries, key_rows, value_rows):

    def single(triple):
        query_head, key_head, value_head = triple
        scores = jnp.dot(query_head, key_head.T, preferred_element_type=jnp.float32)
        maxima = jnp.max(scores, axis=-1, keepdims=True)
        weights = jnp.exp(scores - maxima)
        probability = (weights / jnp.sum(weights, axis=-1, keepdims=True)).astype(jnp.bfloat16)
        return jnp.dot(probability, value_head, preferred_element_type=jnp.float32).astype(
            jnp.bfloat16
        )

    per_head = lax.map(
        single,
        (jnp.swapaxes(queries, 0, 1), jnp.swapaxes(key_rows, 0, 1), jnp.swapaxes(value_rows, 0, 1)),
    )
    return jnp.swapaxes(per_head, 0, 1).reshape(queries.shape[0], -1)


def slot_order(server_list):
    clip_count = server_list.shape[0]
    indices = jnp.arange(clip_count, dtype=jnp.int32)
    earlier = (server_list[None, :] < server_list[:, None]) | (
        server_list[None, :] == server_list[:, None]
    ) & (indices[None, :] < indices[:, None])
    slot_of = jnp.sum(earlier.astype(jnp.int32), axis=1)
    return jnp.sum(jnp.where(slot_of[None, :] == indices[:, None], indices[None, :], 0), axis=1)


def regroup(block_rows, clip_order):
    group_size = lax.axis_size("dp")
    piece_rows = block_rows.reshape(group_size, -1)
    shuffled = lax.all_to_all(piece_rows, "dp", split_axis=0, concat_axis=0, tiled=True)
    picked = jnp.take(shuffled, clip_order, axis=0)
    returned = lax.all_to_all(picked, "dp", split_axis=0, concat_axis=0, tiled=True)
    return returned.reshape(block_rows.shape)


def block_term(operand, weight_rows, row_count, frame_count, local_width):
    blocks = row_count // frame_count
    product = jnp.dot(operand, weight_rows, preferred_element_type=jnp.float32)
    return (
        product.reshape(frame_count, blocks, local_width)
        .transpose(1, 0, 2)
        .reshape(blocks * frame_count, local_width)
    )


def on_device(
    frames_in,
    ln1_gain,
    ln1_bias,
    qkv_weight,
    qv_bias,
    out_weight,
    out_bias,
    ln2_gain,
    ln2_bias,
    fc1_weight,
    fc1_bias,
    fc2_weight,
    fc2_bias,
    server_of_clip,
):
    clip_order = slot_order(server_of_clip)
    group_rows = frames_in.shape[2]
    local_width = frames_in.shape[3] // 4
    frame_count = group_rows * 4
    residual_in = frames_in[0, 0].reshape(frame_count, local_width)
    residual_in = regroup(residual_in, clip_order)
    normed_one = normalize(residual_in, ln1_gain, ln1_bias)
    column_count = qkv_weight.shape[2]
    weight_piece = lax.all_gather(qkv_weight, "dp", axis=0, tiled=True)
    operand = normed_one
    projected = jnp.dot(
        operand, weight_piece.reshape(weight_piece.shape[0], -1), preferred_element_type=jnp.float32
    ).reshape(frame_count, 3, column_count)
    queries = (
        ((projected[:, 0] + qv_bias[0]) * HDIM ** (-0.5))
        .astype(jnp.bfloat16)
        .reshape(frame_count, -1, HDIM)
    )
    key_rows = projected[:, 1].astype(jnp.bfloat16).reshape(frame_count, -1, HDIM)
    value_rows = (projected[:, 2] + qv_bias[1]).astype(jnp.bfloat16).reshape(frame_count, -1, HDIM)
    context = attend(queries, key_rows, value_rows)
    output_rows = lax.all_gather(out_weight, "dp", axis=0, tiled=True)
    carried = residual_in.astype(jnp.float32) + out_bias
    attended = (
        carried
        + lax.psum_scatter(
            block_term(
                context, output_rows, frame_count * lax.axis_size("head"), frame_count, local_width
            ).astype(jnp.bfloat16),
            "head",
            scatter_dimension=0,
            tiled=True,
        ).astype(jnp.float32)
    ).astype(jnp.bfloat16)
    normed_two = normalize(attended, ln2_gain, ln2_bias)
    operand = normed_two
    hidden_sums = jnp.dot(
        operand,
        lax.all_gather(fc1_weight, "dp", axis=0, tiled=True),
        preferred_element_type=jnp.float32,
    )
    hidden = jax.nn.gelu(hidden_sums + fc1_bias, approximate=False).astype(jnp.bfloat16)
    down_rows = lax.all_gather(fc2_weight, "dp", axis=0, tiled=True)
    kept = attended.astype(jnp.float32) + fc2_bias
    layer_out = (
        kept
        + lax.psum_scatter(
            block_term(
                hidden, down_rows, frame_count * lax.axis_size("head"), frame_count, local_width
            ).astype(jnp.bfloat16),
            "head",
            scatter_dimension=0,
            tiled=True,
        ).astype(jnp.float32)
    ).astype(jnp.bfloat16)
    return layer_out.reshape(1, 1, group_rows, 4 * local_width)


def solution(mesh):
    placed = (
        P("dp", "head", None, None),
        P(),
        P(),
        P("dp", None, "head"),
        P(None, "head"),
        P(("head", "dp"), None),
        P("head"),
        P(),
        P(),
        P("dp", "head"),
        P("head"),
        P(("head", "dp"), None),
        P("head"),
        P(),
    )
    return jax.shard_map(
        on_device,
        mesh=mesh,
        in_specs=placed,
        out_specs=P("dp", "head", None, None),
        check_vma=False,
    )
```

profile of v0, /device:TPU:0, one launch (start us, length us, event | category | flops | bytes accessed | tf_op | source)
XLA Modules:
  0.0 602.3 jit_solution(14963864365665853193)
XLA Ops:
  7.3 4.3 all_to_all.16
  12.1 11.7 %reduce.9 = bf16[16,51200]{1,0:T(8,128)(2,1)} reduce(bf16[16,1,51200]{2,1,0:T(2,128)(2,1)S(1)} %all_to_all.16, bf16[]{:T(256)} %broadcast.140), dimensions={1}, to_apply=%all_to_all.16.reduce_sub_computation | reduce | bytes 3276802 | tf_op jit(solution)/shard_map/all_to_all | solution.py:56
  23.7 3.4 reshape.149
  27.1 7.4 %all-to-all-start = ((bf16[16,2,25600]{2,1,0:T(2,128)(2,1)}), bf16[16,2,25600]{2,1,0:T(2,128)(2,1)S(1)}, u32[]{:S(2)}, u32[]{:S(2)}) async-start(bf16[16,2,25600]{2,1,0:T(2,128)(2,1)} %reshape.149), calls=%async_computation | async-start | bytes 3276800 | tf_op jit(solution)/shard_map/all_to_all | solution.py:56
  36.0 36.7 %all-to-all-done = bf16[16,2,25600]{2,1,0:T(2,128)(2,1)S(1)} async-done(((bf16[16,2,25600]{2,1,0:T(2,128)(2,1)}), bf16[16,2,25600]{2,1,0:T(2,128)(2,1)S(1)}, u32[]{:S(2)}, u32[]{:S(2)}) %all-to-all-start) | async-done | bytes 1638432 | tf_op jit(solution)/shard_map/all_to_all | solution.py:56
  72.7 6.2 %reshape.150 = bf16[16,1,51200]{2,1,0:T(2,128)(2,1)} reshape(bf16[16,2,25600]{2,1,0:T(2,128)(2,1)S(1)} %all-to-all-done) | data formatting | bytes 3276800
  78.8 2.9 copy.58
  81.7 2.8 gather_fusion
  89.4 58.1 %all_to_all.19 = bf16[16,2,25600]{2,1,0:T(2,128)(2,1)} all-to-all(bf16[16,2,25600]{2,1,0:T(2,128)(2,1)S(1)} %reshape.151), channel_id=1, replica_groups=mesh['dp'=16,'head'=2] {'dp'}, dimensions={0} | all-to-all | bytes 3276800 | tf_op jit(solution)/shard_map/all_to_all | solution.py:58
  147.4 8.0 %reshape.152 = bf16[16,1,51200]{2,1,0:T(2,128)(2,1)S(1)} reshape(bf16[16,2,25600]{2,1,0:T(2,128)(2,1)} %all_to_all.19) | data formatting | bytes 3276800
  155.4 11.1 %reduce = bf16[16,51200]{1,0:T(8,128)(2,1)} reduce(bf16[16,1,51200]{2,1,0:T(2,128)(2,1)S(1)} %reshape.152, bf16[]{:T(256)} %constant.106), dimensions={1}, to_apply=%all_to_all.15.reduce_sub_computation | reduce | bytes 3276802 | tf_op jit(solution)/shard_map/all_to_all | solution.py:58
  166.6 2.8 reshape.122
  169.8 2.5 copy.51
  172.3 6.4 %copy.47 = bf16[1280,3,512]{0,2,1:T(8,128)(2,1)} copy(bf16[1280,3,512]{2,0,1:T(8,128)(2,1)} %all-gather.9.cloned.1.call-done) | data formatting | bytes 7864320 | tf_op jit(solution)/shard_map/all_gather | solution.py:96
  178.7 36.6 %all-gather.7.cloned.1.call-done = bf16[1280,1280]{1,0:T(8,128)(2,1)} async-done(((bf16[1280,640]{1,0:T(8,128)(2,1)}), bf16[1280,1280]{1,0:T(8,128)(2,1)}) %all-gather.7.cloned.1.call-update) | async-done | bytes 3276816 | tf_op jit(solution)/shard_map/all_gather | solution.py:20
  215.3 2.6 convert_reduce_fusion.1
  217.9 2.9 fusion.32
  220.8 7.8 %fusion.36 = f32[1280,3,512]{0,2,1:T(8,128)S(1)} fusion(bf16[1280,3,512]{0,2,1:T(8,128)(2,1)} %copy.47, bf16[1280,1280]{1,0:T(8,128)(2,1)S(1)} %copy-done.2, f32[1280]{0:T(1024)S(1)} %copy-done.8, f32[1280]{0:T(1024)S(1)} %copy-done.9, f32[1280]{0:T(1024)S(1)} %add_rsqrt_fusion.1, f32[1280]{0:T(1024)S(1)} %broadcast_multiply_fusion.1), kind=kOutput, calls=%fused_computation.57 | convolution fusion | flops 5042995200 | bytes 15093760 | tf_op jit(solution)/shard_map/dot_general | solution.py:98
  231.7 5.0 copy.48
  236.7 3.7 copy.50
  240.4 3.8 copy.49
  244.2 6.8 %fusion.54 = (bf16[8,1280,64]{2,1,0:T(8,128)(2,1)S(1)}, bf16[8,1280,64]{2,1,0:T(8,128)(2,1)}) fusion(f32[1280,8,64]{2,0,1:T(8,128)} %copy.48, f32[8,64]{1,0:T(8,128)S(1)} %add.113, f32[1280,8,64]{2,0,1:T(8,128)} %copy.50, f32[8,64]{1,0:T(8,128)S(1)} %add.116), kind=kLoop, calls=%fused_computation.70 | loop fusion | flops 3276800 | bytes 7868416 | tf_op jit(solution)/shard_map/transpose | solution.py:38
  250.9 47.2 %while.10 = (s32[]{:T(128)}, bf16[8,1280,64]{1,2,0:T(8,128)(2,1)}, bf16[8,1280,64]{2,1,0:T(8,128)(2,1)S(1)}, bf16[8,1280,64]{2,1,0:T(8,128)(2,1)}, bf16[8,1280,64]{2,1,0:T(8,128)(2,1)}, /*index=5*/s32[]{:T(128)}) while((s32[]{:T(128)}, bf16[8,1280,64]{1,2,0:T(8,128)(2,1)}, bf16[8,1280,64]{2,1,0:T(8,128)(2,1)S(1)}, ...), condition=%wide.region_7.8_spmd, body=%wide.region_4.7_spmd.sunk | while | flops 429340160 | bytes 20835396 | solution.py:36
  251.1 2.0 fusion.108
  254.1 2.9 fusion.110
  257.0 2.0 fusion.108
  260.0 2.9 fusion.110
  265.9 2.9 fusion.110
  268.8 2.0 fusion.108
  271.7 2.9 fusion.110
  274.6 2.0 fusion.108
  277.6 2.9 fusion.110
  280.5 2.0 fusion.108
  283.5 2.9 fusion.110
  289.4 2.9 fusion.110
  295.2 2.9 fusion.110
  298.2 5.4 convolution_convert_fusion.1
  303.7 44.9 %reduce-scatter.3.cloned.1.call-done = bf16[1280,640]{1,0:T(8,128)(2,1)} async-done(((bf16[2560,640]{1,0:T(8,128)(2,1)}), bf16[1280,640]{1,0:T(8,128)(2,1)}) %reduce-scatter.3.cloned.1.call-update) | async-done | bytes 1638416 | tf_op jit(solution)/shard_map/reduce_scatter | solution.py:113
  348.6 3.1 add_convert_fusion.2
  353.1 45.2 %all-gather.13.cloned.1.call-done = bf16[1280,1280]{1,0:T(8,128)(2,1)} async-done(((bf16[1280,640]{1,0:T(8,128)(2,1)}), bf16[1280,1280]{1,0:T(8,128)(2,1)}) %all-gather.13.cloned.1.call-update) | async-done | bytes 3276816 | tf_op jit(solution)/shard_map/all_gather | solution.py:20
  398.3 2.6 convert_reduce_fusion
  400.9 2.9 fusion.28
  403.8 59.5 %all-gather.15.cloned.1.call-done = bf16[1280,2560]{1,0:T(8,128)(2,1)} async-done(((bf16[80,2560]{1,0:T(8,128)(2,1)}), bf16[1280,2560]{1,0:T(8,128)(2,1)}) %all-gather.15.cloned.1.call-update) | async-done | bytes 6553616 | tf_op jit(solution)/shard_map/all_gather | solution.py:126
  463.3 40.8 %fusion.16.clone.4 = bf16[1280,2560]{1,0:T(8,128)(2,1)} fusion(f32[2560]{0:T(1024)S(1)} %copy-done.7, bf16[1280,2560]{1,0:T(8,128)(2,1)} %all-gather.15.cloned.1.call-done, bf16[1280,1280]{1,0:T(8,128)(2,1)S(1)} %copy-done.3, f32[1280]{0:T(1024)S(1)} %copy-done.10, f32[1280]{0:T(1024)S(1)} %copy-done.11, f32[1280]{0:T(1024)S(1)} %add_rsqrt_fusion, ...), kind=kOutput, calls=%fused_computation.21.clone.clone.clone.1 | convolution fusion | flops 8614707200 | bytes 16414720 | tf_op jit(solution)/shard_map/dot_general | solution.py:124
  504.1 23.1 %all-gather.17.cloned.1.call-done = bf16[2560,1280]{1,0:T(8,128)(2,1)} async-done(((bf16[160,1280]{1,0:T(8,128)(2,1)}), bf16[2560,1280]{1,0:T(8,128)(2,1)}) %all-gather.17.cloned.1.call-update) | async-done | bytes 6553616 | tf_op jit(solution)/shard_map/all_gather | solution.py:130
  527.2 14.3 %convolution_convert_fusion = bf16[1280,1280]{0,1:T(8,128)(2,1)} fusion(bf16[2560,1280]{1,0:T(8,128)(2,1)} %all-gather.17.cloned.1.call-done, bf16[1280,2560]{1,0:T(8,128)(2,1)} %fusion.16.clone.4), kind=kOutput, calls=%fused_computation.45 | convolution fusion | flops 8390246400 | bytes 16384000 | tf_op jit(solution)/shard_map/dot_general | solution.py:64
  541.5 5.8 copy.53
  547.4 43.8 %reduce-scatter.5.cloned.1.call-done = bf16[1280,640]{1,0:T(8,128)(2,1)} async-done(((bf16[2560,640]{1,0:T(8,128)(2,1)}), bf16[1280,640]{1,0:T(8,128)(2,1)}) %reduce-scatter.5.cloned.1.call-update) | async-done | bytes 1638416 | tf_op jit(solution)/shard_map/reduce_scatter | solution.py:134
  (76 shorter events, 30.0 us)
Async XLA Ops:
  6.5 163.3 %all-gather.11.cloned.1.call-start = ((), (), s32[]{:S(2)}) async-start(), calls=%async_computation.6 | async-start | bytes 1392640 | tf_op jit(solution)/shard_map/all_gather | solution.py:109
  11.6 24.1 %copy-start.12 = (s32[16]{0:T(128)S(1)}, s32[16]{0:T(128)}, u32[]{:S(2)}) copy-start(s32[16]{0:T(128)} %param.29) | copy-start | bytes 196
  27.1 45.6 %all-to-all-start = ((bf16[16,2,25600]{2,1,0:T(2,128)(2,1)}), bf16[16,2,25600]{2,1,0:T(2,128)(2,1)S(1)}, u32[]{:S(2)}, u32[]{:S(2)}) async-start(bf16[16,2,25600]{2,1,0:T(2,128)(2,1)} %reshape.149), calls=%async_computation | async-start | bytes 3276800 | tf_op jit(solution)/shard_map/all_to_all | solution.py:56
  34.5 137.8 %all-gather.9.cloned.1.call-start = ((), (), s32[]{:S(2)}) async-start(), calls=%async_computation.5 | async-start | bytes 4177920 | tf_op jit(solution)/shard_map/all_gather | solution.py:96
  35.3 180.0 %all-gather.7.cloned.1.call-start = ((), (), s32[]{:S(2)}) async-start(), calls=%async_computation.4 | async-start | bytes 4915200 | tf_op jit(solution)/shard_map/all_gather | solution.py:20
  147.4 22.2 %copy-start.4 = (f32[2,512]{1,0:T(2,128)S(1)}, f32[2,512]{1,0:T(2,128)}, u32[]{:S(2)}) copy-start(f32[2,512]{1,0:T(2,128)} %param.20) | copy-start | bytes 12292
  169.4 179.2 %reduce-scatter.3.cloned.1.call-start = ((), (), s32[]{:S(2)}) async-start(), calls=%async_computation.7 | async-start | bytes 4915200 | tf_op jit(solution)/shard_map/reduce_scatter | solution.py:113
  172.3 48.5 %copy-start.8 = (f32[1280]{0:T(1024)S(1)}, f32[1280]{0:T(1024)}, u32[]{:S(2)}) copy-start(f32[1280]{0:T(1024)} %param.18) | copy-start | bytes 15364
  172.3 48.6 %copy-start.9 = (f32[1280]{0:T(1024)S(1)}, f32[1280]{0:T(1024)}, u32[]{:S(2)}) copy-start(f32[1280]{0:T(1024)} %param.17) | copy-start | bytes 15364
  215.3 5.5 copy-start.2
  298.2 50.5 %copy-start = (bf16[1280,640]{1,0:T(8,128)(2,1)S(1)}, bf16[1280,640]{1,0:T(8,128)(2,1)}, u32[]{:S(2)}) copy-start(bf16[1280,640]{1,0:T(8,128)(2,1)} %reshape.122) | copy-start | bytes 4915204
  298.2 50.5 %copy-start.5 = (f32[640]{0:T(1024)S(1)}, f32[640]{0:T(1024)}, u32[]{:S(2)}) copy-start(f32[640]{0:T(1024)} %param.22) | copy-start | bytes 7684
  303.6 159.7 %copy-start.7 = (f32[2560]{0:T(1024)S(1)}, f32[2560]{0:T(1024)}, u32[]{:S(2)}) copy-start(f32[2560]{0:T(1024)} %param.26) | copy-start | bytes 30724
  303.6 159.7 %copy-start.10 = (f32[1280]{0:T(1024)S(1)}, f32[1280]{0:T(1024)}, u32[]{:S(2)}) copy-start(f32[1280]{0:T(1024)} %param.24) | copy-start | bytes 15364
  303.6 159.7 %copy-start.11 = (f32[1280]{0:T(1024)S(1)}, f32[1280]{0:T(1024)}, u32[]{:S(2)}) copy-start(f32[1280]{0:T(1024)} %param.23) | copy-start | bytes 15364
  303.7 94.6 %all-gather.13.cloned.1.call-start = ((), (), s32[]{:S(2)}) async-start(), calls=%async_computation.8 | async-start | bytes 4915200 | tf_op jit(solution)/shard_map/all_gather | solution.py:20
  351.7 111.6 %all-gather.15.cloned.1.call-start = ((), (), s32[]{:S(2)}) async-start(), calls=%async_computation.9 | async-start | bytes 6963200 | tf_op jit(solution)/shard_map/all_gather | solution.py:126
  352.3 174.9 %all-gather.17.cloned.1.call-start = ((), (), s32[]{:S(2)}) async-start(), calls=%async_computation.10 | async-start | bytes 6963200 | tf_op jit(solution)/shard_map/all_gather | solution.py:130
  353.1 238.1 %reduce-scatter.5.cloned.1.call-start = ((), (), s32[]{:S(2)}) async-start(), calls=%async_computation.11 | async-start | bytes 4915200 | tf_op jit(solution)/shard_map/reduce_scatter | solution.py:134
  398.3 65.0 %copy-start.3 = (bf16[1280,1280]{1,0:T(8,128)(2,1)S(1)}, bf16[1280,1280]{1,0:T(8,128)(2,1)}, u32[]{:S(2)}) copy-start(bf16[1280,1280]{1,0:T(8,128)(2,1)} %all-gather.13.cloned.1.call-done) | copy-start | bytes 9830404
  541.5 49.6 %copy-start.1 = (bf16[1280,640]{1,0:T(8,128)(2,1)S(1)}, bf16[1280,640]{1,0:T(8,128)(2,1)}, u32[]{:S(2)}) copy-start(bf16[1280,640]{1,0:T(8,128)(2,1)} %add_convert_fusion.2) | copy-start | bytes 4915204
  541.5 49.6 %copy-start.6 = (f32[640]{0:T(1024)S(1)}, f32[640]{0:T(1024)}, u32[]{:S(2)}) copy-start(f32[640]{0:T(1024)} %param.28) | copy-start | bytes 7684
Sparse Core Ops, SparseCore 0:
  9.6 48.2 all-gather.10
  60.2 57.7 all-gather.8
  169.5 45.7 all-gather.6
  303.7 44.8 reduce-scatter.2
  351.9 46.3 all-gather.12
  400.4 62.8 all-gather.14
  465.6 61.5 all-gather.16
  547.5 43.6 reduce-scatter.4
where the time goes:
time: 612 us; the launch traced here: 602 us
  waiting for transfers between devices  292 us (48%)
  matrix products  108 us (18%)
  local copies, waits for them, and re-layouts  64.6 us (11%)
  blocking collectives  58.1 us (9%)
  other arithmetic  57.1 us (9%)
  between operations  14.2 us (2%)
  starting transfers between devices  8.18 us (1%)
    all_gather x2, waiting for transfers between devices, normalize(): whole_rows = lax.all_gather(residual_in, 'head', axis=1, tiled=True)  81.8 us
    all_gather x1, waiting for transfers between devices, on_device(): lax.all_gather(fc1_weight, 'dp', axis=0, tiled=True)  59.5 us
    all_to_all x1, blocking collectives, regroup(): lax.all_to_all(picked, 'dp', split_axis=0, concat_axis=0, tiled=True)  58.1 us
    reduce_scatter x1, waiting for transfers between devices, on_device(): lax.psum_scatter(block_term(context, output_rows, frame_count * lax.axis_...  44.9 us
    reduce_scatter x1, waiting for transfers between devices, on_device(): lax.psum_scatter(block_term(hidden, down_rows, frame_count * lax.axis_siz...  43.8 us
    dot_general x1, matrix products, on_device(): jnp.dot(operand, lax.all_gather(fc1_weight, 'dp', axis=0, tiled=True), pr...  40.8 us
    all_to_all x1, waiting for transfers between devices, regroup(): lax.all_to_all(piece_rows, 'dp', split_axis=0, concat_axis=0, tiled=True)  36.7 us
    dot_general x8, matrix products, single(): jnp.dot(probability, value_head, preferred_element_type=jnp.float32)  23.2 us
  transfers between devices with their start and end apart: 9, of which 7 were waited for; matrix products, arithmetic and copies ran while one was open for 18% of the time, Pallas kernels for 0%

commit v1 on v0

--- a/solution.py
+++ b/solution.py
@@ -123,7 +123,9 @@
     operand = normed_two
     hidden_sums = jnp.dot(
         operand,
-        lax.all_gather(fc1_weight, "dp", axis=0, tiled=True),
+        jnp.concatenate(
+            lax.all_to_all(jnp.stack([fc1_weight] * lax.axis_size("dp")), "dp", 0, 0), axis=0
+        ),
         preferred_element_type=jnp.float32,
     )
     hidden = jax.nn.gelu(hidden_sums + fc1_bias, approximate=False).astype(jnp.bfloat16)

time: 612 us -> 549 us (0.90)
  waiting for transfers between devices: 292 us -> 220 us
    all_gather x1 -> x0, waiting for transfers between devices: 59.5 us -> none  [on_device(): lax.all_gather(fc1_weight, 'dp', axis=0, tiled=True)]
    all_gather x2, waiting for transfers between devices: 81.8 us -> 73.5 us  [normalize(): whole_rows = lax.all_gather(residual_in, 'head', axis=1, tiled=True)]
  transfers between devices with their start and end apart: 9 -> 9, of which waited for: 7 -> 6; matrix products, arithmetic and copies ran while one was open for 18% -> 38% of each run, Pallas kernels for 0% -> 0%
where the time goes in v1:
time: 549 us; the launch traced here: 538 us
  waiting for transfers between devices  220 us (40%)
  matrix products  107 us (19%)
  local copies, waits for them, and re-layouts  68.7 us (13%)
  blocking collectives  58 us (11%)
  other arithmetic  57.1 us (10%)
  between operations  14.2 us (3%)
  starting transfers between devices  13 us (2%)
    all_gather x2, waiting for transfers between devices, normalize(): whole_rows = lax.all_gather(residual_in, 'head', axis=1, tiled=True)  73.5 us
    all_to_all x1, blocking collectives, regroup(): lax.all_to_all(picked, 'dp', split_axis=0, concat_axis=0, tiled=True)  58 us
    reduce_scatter x1, waiting for transfers between devices, on_device(): lax.psum_scatter(block_term(context, output_rows, frame_count * lax.axis_...  44.9 us
    reduce_scatter x1, waiting for transfers between devices, on_device(): lax.psum_scatter(block_term(hidden, down_rows, frame_count * lax.axis_siz...  43.8 us
    dot_general x1, matrix products, on_device(): jnp.dot(operand, jnp.concatenate(lax.all_to_all(jnp.stack([fc1_weight] *...  40.8 us
    all_to_all x1, waiting for transfers between devices, regroup(): lax.all_to_all(piece_rows, 'dp', split_axis=0, concat_axis=0, tiled=True)  36.7 us
    dot_general x8, matrix products, single(): jnp.dot(probability, value_head, preferred_element_type=jnp.float32)  23.2 us
    unnamed x31, local copies, waits for them, and re-layouts  21.9 us
  transfers between devices with their start and end apart: 9, of which 6 were waited for; matrix products, arithmetic and copies ran while one was open for 38% of the time, Pallas kernels for 0%

profile of v1, /device:TPU:0, one launch (start us, length us, event | category | flops | bytes accessed | tf_op | source)
XLA Modules:
  0.0 538.3 jit_solution(9228253219716900360)
XLA Ops:
  7.3 4.3 all_to_all.20
  12.1 11.7 %reduce.9 = bf16[16,51200]{1,0:T(8,128)(2,1)} reduce(bf16[16,1,51200]{2,1,0:T(2,128)(2,1)S(1)} %all_to_all.20, bf16[]{:T(256)} %broadcast.142), dimensions={1}, to_apply=%all_to_all.20.reduce_sub_computation | reduce | bytes 3276802 | tf_op jit(solution)/shard_map/all_to_all | solution.py:56
  23.8 3.4 reshape.155
  27.2 7.4 %all-to-all-start = ((bf16[16,2,25600]{2,1,0:T(2,128)(2,1)}), bf16[16,2,25600]{2,1,0:T(2,128)(2,1)S(1)}, u32[]{:S(2)}, u32[]{:S(2)}) async-start(bf16[16,2,25600]{2,1,0:T(2,128)(2,1)} %reshape.155), calls=%async_computation | async-start | bytes 3276800 | tf_op jit(solution)/shard_map/all_to_all | solution.py:56
  36.0 36.7 %all-to-all-done = bf16[16,2,25600]{2,1,0:T(2,128)(2,1)S(1)} async-done(((bf16[16,2,25600]{2,1,0:T(2,128)(2,1)}), bf16[16,2,25600]{2,1,0:T(2,128)(2,1)S(1)}, u32[]{:S(2)}, u32[]{:S(2)}) %all-to-all-start) | async-done | bytes 1638432 | tf_op jit(solution)/shard_map/all_to_all | solution.py:56
  72.7 6.2 %reshape.156 = bf16[16,1,51200]{2,1,0:T(2,128)(2,1)} reshape(bf16[16,2,25600]{2,1,0:T(2,128)(2,1)S(1)} %all-to-all-done) | data formatting | bytes 3276800
  78.9 2.9 copy.58
  81.8 2.8 gather_fusion
  89.5 58.0 %all_to_all.24 = bf16[16,2,25600]{2,1,0:T(2,128)(2,1)} all-to-all(bf16[16,2,25600]{2,1,0:T(2,128)(2,1)S(1)} %reshape.157), channel_id=1, replica_groups=mesh['dp'=16,'head'=2] {'dp'}, dimensions={0} | all-to-all | bytes 3276800 | tf_op jit(solution)/shard_map/all_to_all | solution.py:58
  147.5 8.0 %reshape.158 = bf16[16,1,51200]{2,1,0:T(2,128)(2,1)S(1)} reshape(bf16[16,2,25600]{2,1,0:T(2,128)(2,1)} %all_to_all.24) | data formatting | bytes 3276800
  155.5 11.1 %reduce = bf16[16,51200]{1,0:T(8,128)(2,1)} reduce(bf16[16,1,51200]{2,1,0:T(2,128)(2,1)S(1)} %reshape.158, bf16[]{:T(256)} %constant.106), dimensions={1}, to_apply=%all_to_all.18.reduce_sub_computation | reduce | bytes 3276802 | tf_op jit(solution)/shard_map/all_to_all | solution.py:58
  166.6 2.9 reshape.127
  169.5 4.3 stack.2
  173.8 4.8 all-to-all-start.2
  179.1 2.5 copy.51
  181.6 6.2 %copy.47 = bf16[1280,3,512]{0,2,1:T(8,128)(2,1)} copy(bf16[1280,3,512]{2,0,1:T(8,128)(2,1)} %all-gather.8.cloned.1.call-done) | data formatting | bytes 7864320 | tf_op jit(solution)/shard_map/all_gather | solution.py:96
  187.8 27.6 %all-gather.6.cloned.1.call-done = bf16[1280,1280]{1,0:T(8,128)(2,1)} async-done(((bf16[1280,640]{1,0:T(8,128)(2,1)}), bf16[1280,1280]{1,0:T(8,128)(2,1)}) %all-gather.6.cloned.1.call-update) | async-done | bytes 3276816 | tf_op jit(solution)/shard_map/all_gather | solution.py:20
  215.4 2.6 convert_reduce_fusion.1
  218.0 2.9 fusion.32
  220.9 7.8 %fusion.36 = f32[1280,3,512]{0,2,1:T(8,128)S(1)} fusion(bf16[1280,3,512]{0,2,1:T(8,128)(2,1)} %copy.47, bf16[1280,1280]{1,0:T(8,128)(2,1)S(1)} %copy-done.2, f32[1280]{0:T(1024)S(1)} %copy-done.8, f32[1280]{0:T(1024)S(1)} %copy-done.9, f32[1280]{0:T(1024)S(1)} %add_rsqrt_fusion.1, f32[1280]{0:T(1024)S(1)} %broadcast_multiply_fusion.1), kind=kOutput, calls=%fused_computation.57 | convolution fusion | flops 5042995200 | bytes 15093760 | tf_op jit(solution)/shard_map/dot_general | solution.py:98
  231.7 5.0 copy.48
  236.7 3.7 copy.50
  240.4 3.8 copy.49
  244.2 6.8 %fusion.54 = (bf16[8,1280,64]{2,1,0:T(8,128)(2,1)S(1)}, bf16[8,1280,64]{2,1,0:T(8,128)(2,1)}) fusion(f32[1280,8,64]{2,0,1:T(8,128)} %copy.48, f32[8,64]{1,0:T(8,128)S(1)} %add.113, f32[1280,8,64]{2,0,1:T(8,128)} %copy.50, f32[8,64]{1,0:T(8,128)S(1)} %add.116), kind=kLoop, calls=%fused_computation.70 | loop fusion | flops 3276800 | bytes 7868416 | tf_op jit(solution)/shard_map/transpose | solution.py:38
  251.0 47.2 %while.10 = (s32[]{:T(128)}, bf16[8,1280,64]{1,2,0:T(8,128)(2,1)}, bf16[8,1280,64]{2,1,0:T(8,128)(2,1)S(1)}, bf16[8,1280,64]{2,1,0:T(8,128)(2,1)}, bf16[8,1280,64]{2,1,0:T(8,128)(2,1)}, /*index=5*/s32[]{:T(128)}) while((s32[]{:T(128)}, bf16[8,1280,64]{1,2,0:T(8,128)(2,1)}, bf16[8,1280,64]{2,1,0:T(8,128)(2,1)S(1)}, ...), condition=%wide.region_7.8_spmd, body=%wide.region_4.7_spmd.sunk | while | flops 429340160 | bytes 20835396 | solution.py:36
  254.2 2.9 fusion.110
  260.0 2.9 fusion.110
  263.0 2.0 fusion.108
  265.9 2.9 fusion.110
  271.8 2.9 fusion.110
  274.7 2.0 fusion.108
  277.7 2.9 fusion.110
  280.6 2.0 fusion.108
  283.6 2.9 fusion.110
  286.5 2.0 fusion.108
  289.4 2.9 fusion.110
  295.3 2.9 fusion.110
  298.2 5.4 %convolution_convert_fusion.1 = bf16[1280,2,640]{2,0,1:T(8,128)(2,1)} fusion(bf16[1280,512,1]{0,1,2:T(8,128)(2,1)} %bitcast.19, bf16[2,640,512]{2,1,0:T(8,128)(2,1)} %bitcast.87), kind=kOutput, calls=%fused_computation.56 | convolution fusion | flops 1679360000 | bytes 5898240 | tf_op jit(solution)/shard_map/dot_general | solution.py:64
  303.8 44.9 %reduce-scatter.3.cloned.1.call-done = bf16[1280,640]{1,0:T(8,128)(2,1)} async-done(((bf16[2560,640]{1,0:T(8,128)(2,1)}), bf16[1280,640]{1,0:T(8,128)(2,1)}) %reduce-scatter.3.cloned.1.call-update) | async-done | bytes 1638416 | tf_op jit(solution)/shard_map/reduce_scatter | solution.py:113
  348.7 3.1 add_convert_fusion.2
  352.4 45.9 %all-gather.12.cloned.1.call-done = bf16[1280,1280]{1,0:T(8,128)(2,1)} async-done(((bf16[1280,640]{1,0:T(8,128)(2,1)}), bf16[1280,1280]{1,0:T(8,128)(2,1)}) %all-gather.12.cloned.1.call-update) | async-done | bytes 3276816 | tf_op jit(solution)/shard_map/all_gather | solution.py:20
  398.4 2.6 convert_reduce_fusion
  400.9 2.9 fusion.28
  403.9 40.8 %fusion.16.clone.4 = bf16[1280,2560]{1,0:T(8,128)(2,1)} fusion(f32[2560]{0:T(1024)S(1)} %copy-done.7, bf16[1280,2560]{1,0:T(8,128)(2,1)} %bitcast.24, bf16[1280,1280]{1,0:T(8,128)(2,1)S(1)} %copy-done.3, f32[1280]{0:T(1024)S(1)} %copy-done.10, f32[1280]{0:T(1024)S(1)} %copy-done.11, f32[1280]{0:T(1024)S(1)} %add_rsqrt_fusion, ...), kind=kOutput, calls=%fused_computation.21.clone.clone.clone.1 | convolution fusion | flops 8614707200 | bytes 16414720 | tf_op jit(solution)/shard_map/dot_general | solution.py:124
  444.7 18.6 %all-gather.14.cloned.1.call-done = bf16[2560,1280]{1,0:T(8,128)(2,1)} async-done(((bf16[160,1280]{1,0:T(8,128)(2,1)}), bf16[2560,1280]{1,0:T(8,128)(2,1)}) %all-gather.14.cloned.1.call-update) | async-done | bytes 6553616 | tf_op jit(solution)/shard_map/all_gather | solution.py:132
  463.4 14.3 %convolution_convert_fusion = bf16[1280,1280]{0,1:T(8,128)(2,1)} fusion(bf16[2560,1280]{1,0:T(8,128)(2,1)} %all-gather.14.cloned.1.call-done, bf16[1280,2560]{1,0:T(8,128)(2,1)} %fusion.16.clone.4), kind=kOutput, calls=%fused_computation.45 | convolution fusion | flops 8390246400 | bytes 16384000 | tf_op jit(solution)/shard_map/dot_general | solution.py:64
  477.6 5.7 %copy.53 = bf16[2,1280,640]{2,1,0:T(8,128)(2,1)} copy(bf16[2,1280,640]{1,2,0:T(8,128)(2,1)} %bitcast.85) | data formatting | bytes 6553600 | tf_op jit(solution)/shard_map/convert_element_type | solution.py:139
  483.4 43.8 %reduce-scatter.5.cloned.1.call-done = bf16[1280,640]{1,0:T(8,128)(2,1)} async-done(((bf16[2560,640]{1,0:T(8,128)(2,1)}), bf16[1280,640]{1,0:T(8,128)(2,1)}) %reduce-scatter.5.cloned.1.call-update) | async-done | bytes 1638416 | tf_op jit(solution)/shard_map/reduce_scatter | solution.py:136
  (76 shorter events, 31.2 us)
Async XLA Ops:
  6.5 172.5 %all-gather.10.cloned.1.call-start = ((), (), s32[]{:S(2)}) async-start(), calls=%async_computation.7 | async-start | bytes 1392640 | tf_op jit(solution)/shard_map/all_gather | solution.py:109
  11.6 24.1 %copy-start.12 = (s32[16]{0:T(128)S(1)}, s32[16]{0:T(128)}, u32[]{:S(2)}) copy-start(s32[16]{0:T(128)} %param.29) | copy-start | bytes 196
  27.2 45.6 %all-to-all-start = ((bf16[16,2,25600]{2,1,0:T(2,128)(2,1)}), bf16[16,2,25600]{2,1,0:T(2,128)(2,1)S(1)}, u32[]{:S(2)}, u32[]{:S(2)}) async-start(bf16[16,2,25600]{2,1,0:T(2,128)(2,1)} %reshape.155), calls=%async_computation | async-start | bytes 3276800 | tf_op jit(solution)/shard_map/all_to_all | solution.py:56
  34.6 147.0 %all-gather.8.cloned.1.call-start = ((), (), s32[]{:S(2)}) async-start(), calls=%async_computation.6 | async-start | bytes 4177920 | tf_op jit(solution)/shard_map/all_gather | solution.py:96
  35.3 180.1 %all-gather.6.cloned.1.call-start = ((), (), s32[]{:S(2)}) async-start(), calls=%async_computation.5 | async-start | bytes 4915200 | tf_op jit(solution)/shard_map/all_gather | solution.py:20
  173.8 5.1 copy-start.4
  173.8 230.0 %all-to-all-start.2 = ((bf16[16,80,2560]{2,1,0:T(8,128)(2,1)}), bf16[16,80,2560]{2,1,0:T(8,128)(2,1)}, u32[]{:S(2)}, u32[]{:S(2)}) async-start(bf16[16,80,2560]{2,1,0:T(8,128)(2,1)} %stack.2), calls=%async_computation.3 | async-start | bytes 13107200 | tf_op jit(solution)/shard_map/all_to_all | solution.py:127
  178.6 170.0 %reduce-scatter.3.cloned.1.call-start = ((), (), s32[]{:S(2)}) async-start(), calls=%async_computation.8 | async-start | bytes 4915200 | tf_op jit(solution)/shard_map/reduce_scatter | solution.py:113
  181.6 39.4 %copy-start.8 = (f32[1280]{0:T(1024)S(1)}, f32[1280]{0:T(1024)}, u32[]{:S(2)}) copy-start(f32[1280]{0:T(1024)} %param.18) | copy-start | bytes 15364
  181.6 39.4 %copy-start.9 = (f32[1280]{0:T(1024)S(1)}, f32[1280]{0:T(1024)}, u32[]{:S(2)}) copy-start(f32[1280]{0:T(1024)} %param.17) | copy-start | bytes 15364
  215.4 5.5 %copy-start.2 = (bf16[1280,1280]{1,0:T(8,128)(2,1)S(1)}, bf16[1280,1280]{1,0:T(8,128)(2,1)}, u32[]{:S(2)}) copy-start(bf16[1280,1280]{1,0:T(8,128)(2,1)} %all-gather.6.cloned.1.call-done) | copy-start | bytes 9830404
  298.2 50.5 %copy-start = (bf16[1280,640]{1,0:T(8,128)(2,1)S(1)}, bf16[1280,640]{1,0:T(8,128)(2,1)}, u32[]{:S(2)}) copy-start(bf16[1280,640]{1,0:T(8,128)(2,1)} %reshape.127) | copy-start | bytes 4915204
  298.2 50.5 %copy-start.5 = (f32[640]{0:T(1024)S(1)}, f32[640]{0:T(1024)}, u32[]{:S(2)}) copy-start(f32[640]{0:T(1024)} %param.22) | copy-start | bytes 7684
  303.7 100.2 %copy-start.7 = (f32[2560]{0:T(1024)S(1)}, f32[2560]{0:T(1024)}, u32[]{:S(2)}) copy-start(f32[2560]{0:T(1024)} %param.26) | copy-start | bytes 30724
  303.7 100.2 %copy-start.10 = (f32[1280]{0:T(1024)S(1)}, f32[1280]{0:T(1024)}, u32[]{:S(2)}) copy-start(f32[1280]{0:T(1024)} %param.24) | copy-start | bytes 15364
  303.7 100.2 %copy-start.11 = (f32[1280]{0:T(1024)S(1)}, f32[1280]{0:T(1024)}, u32[]{:S(2)}) copy-start(f32[1280]{0:T(1024)} %param.23) | copy-start | bytes 15364
  303.7 94.6 %all-gather.12.cloned.1.call-start = ((), (), s32[]{:S(2)}) async-start(), calls=%async_computation.9 | async-start | bytes 4915200 | tf_op jit(solution)/shard_map/all_gather | solution.py:20
  351.8 111.5 %all-gather.14.cloned.1.call-start = ((), (), s32[]{:S(2)}) async-start(), calls=%async_computation.10 | async-start | bytes 6963200 | tf_op jit(solution)/shard_map/all_gather | solution.py:132
  352.4 174.8 %reduce-scatter.5.cloned.1.call-start = ((), (), s32[]{:S(2)}) async-start(), calls=%async_computation.11 | async-start | bytes 4915200 | tf_op jit(solution)/shard_map/reduce_scatter | solution.py:136
  398.3 5.6 %copy-start.3 = (bf16[1280,1280]{1,0:T(8,128)(2,1)S(1)}, bf16[1280,1280]{1,0:T(8,128)(2,1)}, u32[]{:S(2)}) copy-start(bf16[1280,1280]{1,0:T(8,128)(2,1)} %all-gather.12.cloned.1.call-done) | copy-start | bytes 9830404
  477.6 49.5 %copy-start.1 = (bf16[1280,640]{1,0:T(8,128)(2,1)S(1)}, bf16[1280,640]{1,0:T(8,128)(2,1)}, u32[]{:S(2)}) copy-start(bf16[1280,640]{1,0:T(8,128)(2,1)} %add_convert_fusion.2) | copy-start | bytes 4915204
  477.6 49.5 %copy-start.6 = (f32[640]{0:T(1024)S(1)}, f32[640]{0:T(1024)}, u32[]{:S(2)}) copy-start(f32[640]{0:T(1024)} %param.28) | copy-start | bytes 7684
Sparse Core Ops, SparseCore 0:
  9.6 48.2 all-gather.9
  60.2 57.7 all-gather.7
  169.6 45.7 all-gather.5
  303.8 44.8 reduce-scatter.2
  351.9 46.3 all-gather.11
  400.5 62.8 all-gather.13
  483.5 43.6 reduce-scatter.4
